TPU v7x, 32 devices: a whole 2x2x4 slice. The times are simulated.
32 devices in a mesh: row: 16 (over z, y, x), col: 2 (over core).
Axes of the slice: x: 2, y: 2, z: 4, core: 2. Of those that a mesh axis runs over, the one named last changes fastest.
Arguments:
- messages: float32 [32, 16, 2, 16, 128], P(('row', 'col')), may hold values from -6 to 6
- dst_local: int32 [32, 16, 2, 16], P(('row', 'col')), may hold values from 0 to 255
- counts: int32 [32, 16, 2], P(('row', 'col')), may hold values from 8 to 16, as said below
- degrees: int32 [8192], P(('row', 'col')), may hold values from 1 to 8
Outputs:
- aggregate: float32 [8192, 128], P(('row', 'col'))
Inputs may be any that keep to these rules, and one draw needn't show every extreme that they name: For every sender and group, the counts over the group's 2 ranges sum to exactly 24. In each group one range receives 16 live slots from every sender.
All inputs are finite; a program needn't handle non-finite values.
Results may differ from a plain program's by a relative error of at most 0.0003.
Values sent between devices are 32-bit elements; how exact they have to be, the bound alone decides.
No kernel may reach another device: no remote copies, remote signals or barrier semaphores. Data moves between devices by JAX's collectives and lax.ppermute only.
A program may use at most 64 MiB of HBM per device.

v0:
```python
import jax
import jax.numpy as jnp
from jax import lax
from jax.sharding import PartitionSpec as P


def body(messages, dst_local, counts, degrees):
    slots = messages.shape[3]
    width = messages.shape[4]
    owned = degrees.shape[0]
    slot_index = lax.broadcasted_iota(jnp.int32, counts.shape + (slots,), 3)
    alive_int = (slot_index < counts[..., None]).astype(jnp.int32)
    alive_mask = alive_int.astype(jnp.float32)
    masked = messages * alive_mask[..., None]
    received, labels = (
        lax.all_to_all(
            lax.all_to_all(masked, "row", split_axis=1, concat_axis=0, tiled=True),
            "col",
            split_axis=2,
            concat_axis=1,
            tiled=True,
        ),
        lax.all_to_all(
            lax.all_to_all(dst_local, "row", split_axis=1, concat_axis=0, tiled=True),
            "col",
            split_axis=2,
            concat_axis=1,
            tiled=True,
        ),
    )
    summed = jax.ops.segment_sum(
        received.reshape(-1, width), labels.reshape(-1), num_segments=owned
    )
    scale = jnp.maximum(degrees, 1).astype(jnp.float32)
    return summed / scale[:, None]


def solution(mesh):
    in_specs = (
        P(("row", "col"), None, None, None, None),
        P(("row", "col"), None, None, None),
        P(("row", "col"), None, None),
        P(("row", "col")),
    )
    out_specs = P(("row", "col"), None)
    return jax.shard_map(body, mesh=mesh, in_specs=in_specs, out_specs=out_specs, check_vma=False)
```

profile of v0, /device:TPU:0, one launch (start us, length us, event | category | flops | bytes accessed | tf_op | source)
XLA Modules:
  0.0 40.6 jit_solution(9112248974094976545)
XLA Ops:
  0.0 8.3 %all-to-all-start = ((s32[1,16,2,16]{3,2,0,1:T(2,128)}), s32[1,16,2,16]{3,2,0,1:T(2,128)S(1)}, u32[]{:S(2)}, u32[]{:S(2)}) async-start(s32[1,16,2,16]{3,2,0,1:T(2,128)} %bitcast.18), calls=%async_computation | async-start | bytes 32768 | tf_op jit(solution)/shard_map/all_to_all | solution.py:24
  8.3 0.0 copy-start
  8.4 0.7 %copy-done = s32[1,16,2]{1,2,0:T(2,128)S(1)} copy-done((s32[1,16,2]{1,2,0:T(2,128)S(1)}, s32[1,16,2]{1,2,0:T(2,128)}, u32[]{:S(2)}) %copy-start) | copy-done | bytes 152
  9.0 0.1 copy.15
  9.1 0.1 fusion.2
  9.2 1.8 %bitcast_multiply_fusion = f32[1,16,2,16,128]{4,3,2,0,1:T(8,128)} fusion(f32[1,16,2,16,128]{4,3,2,1,0:T(8,128)} %param.4, f32[16,2,16]{2,1,0:T(2,128)S(1)} %fusion.2), kind=kLoop, calls=%fused_computation.1 | loop fusion | flops 65536 | bytes 526336 | tf_op jit(solution)/shard_map/mul | solution.py:14
  11.0 4.7 %all-to-all-done = s32[1,16,2,16]{3,2,0,1:T(2,128)S(1)} async-done(((s32[1,16,2,16]{3,2,0,1:T(2,128)}), s32[1,16,2,16]{3,2,0,1:T(2,128)S(1)}, u32[]{:S(2)}, u32[]{:S(2)}) %all-to-all-start) | async-done | bytes 2080 | tf_op jit(solution)/shard_map/all_to_all | solution.py:24
  15.7 0.1 reshape.45
  15.8 3.7 %all_to_all.42 = s32[2,1,256]{2,1,0:T(1,128)S(1)} all-to-all(s32[2,1,256]{2,1,0:T(1,128)S(1)} %reshape.45), channel_id=1, replica_groups=mesh['row'=16,'col'=2] {'col'}, dimensions={0} | all-to-all | bytes 4096 | tf_op jit(solution)/shard_map/all_to_all | solution.py:23
  19.5 0.0 copy-start.1
  19.5 3.7 %all-to-all-start.2 = ((f32[1,16,2,16,128]{4,3,2,0,1:T(8,128)}), f32[1,16,2,16,128]{4,3,2,0,1:T(8,128)S(1)}, u32[]{:S(2)}, u32[]{:S(2)}) async-start(f32[1,16,2,16,128]{4,3,2,0,1:T(8,128)} %bitcast_multiply_fusion), calls=%async_computation.2 | async-start | bytes 524288 | tf_op jit(solution)/shard_map/all_to_all | solution.py:17
  23.1 0.0 copy-done.1
  23.2 0.5 %broadcast.9 = s32[]{:T(128)} broadcast(s32[]{:T(128)} %constant.8), dimensions={} | broadcast | bytes 8 | tf_op jit(solution)/shard_map/all_to_all | solution.py:23
  23.7 0.7 %reduce = s32[2,256]{1,0:T(2,128)S(1)} reduce(s32[2,1,256]{2,1,0:T(1,128)S(1)} %all_to_all.42, s32[]{:T(128)} %broadcast.9), dimensions={1}, to_apply=%all_to_all.14.reduce_sub_computation | reduce | bytes 4100 | tf_op jit(solution)/shard_map/all_to_all | solution.py:23
  24.3 0.1 reshape.46
  24.4 0.1 reshape.36
  24.5 9.0 %all-to-all-done.2 = f32[1,16,2,16,128]{4,3,2,0,1:T(8,128)S(1)} async-done(((f32[1,16,2,16,128]{4,3,2,0,1:T(8,128)}), f32[1,16,2,16,128]{4,3,2,0,1:T(8,128)S(1)}, u32[]{:S(2)}, u32[]{:S(2)}) %all-to-all-start.2) | async-done | bytes 262176 | tf_op jit(solution)/shard_map/all_to_all | solution.py:17
  33.6 3.9 %all_to_all.43 = f32[16,1,2,16,128]{4,3,0,1,2:T(8,128)S(1)} all-to-all(f32[16,1,2,16,128]{4,3,0,1,2:T(8,128)S(1)} %copy.17), channel_id=1, replica_groups=mesh['row'=16,'col'=2] {'col'}, dimensions={2} | all-to-all | bytes 524288 | tf_op jit(solution)/shard_map/all_to_all | solution.py:16
  37.5 2.3 %scatter_custom_fusion = f32[256,128]{1,0:T(8,128)S(1)} fusion(s32[512]{0:T(512)S(1)} %reshape.36, f32[512,128]{1,0:T(8,128)S(1)} %bitcast.14, f32[]{:T(128)} %constant.0.clone.1), kind=kCustom, calls=%fused_computation.3 | custom fusion | flops 65536 | bytes 131076 | tf_op jit(solution)/shard_map/scatter-add | solution.py:31
  39.8 0.8 %broadcast_divide_fusion = f32[256,128]{1,0:T(8,128)} fusion(f32[256,128]{1,0:T(8,128)S(1)} %scatter_custom_fusion, f32[256]{0:T(256)S(1)} %maximum_convert_fusion), kind=kLoop, calls=%fused_computation.2 | loop fusion | flops 32768 | bytes 263168 | tf_op jit(solution)/shard_map/div | solution.py:35
  (5 shorter events, 0.1 us)
Async XLA Ops:
  0.0 15.7 %all-to-all-start = ((s32[1,16,2,16]{3,2,0,1:T(2,128)}), s32[1,16,2,16]{3,2,0,1:T(2,128)S(1)}, u32[]{:S(2)}, u32[]{:S(2)}) async-start(s32[1,16,2,16]{3,2,0,1:T(2,128)} %bitcast.18), calls=%async_computation | async-start | bytes 32768 | tf_op jit(solution)/shard_map/all_to_all | solution.py:24
  8.3 0.7 %copy-start = (s32[1,16,2]{1,2,0:T(2,128)S(1)}, s32[1,16,2]{1,2,0:T(2,128)}, u32[]{:S(2)}) copy-start(s32[1,16,2]{1,2,0:T(2,128)} %param.6) | copy-start | bytes 388
  19.5 3.7 %copy-start.1 = (s32[256]{0:T(256)S(1)}, s32[256]{0:T(256)}, u32[]{:S(2)}) copy-start(s32[256]{0:T(256)} %param.7) | copy-start | bytes 3076
  19.5 14.1 %all-to-all-start.2 = ((f32[1,16,2,16,128]{4,3,2,0,1:T(8,128)}), f32[1,16,2,16,128]{4,3,2,0,1:T(8,128)S(1)}, u32[]{:S(2)}, u32[]{:S(2)}) async-start(f32[1,16,2,16,128]{4,3,2,0,1:T(8,128)} %bitcast_multiply_fusion), calls=%async_computation.2 | async-start | bytes 524288 | tf_op jit(solution)/shard_map/all_to_all | solution.py:17
where the time goes:
time: 41 us; the launch traced here: 40.6 us
  waiting for transfers between devices  13.7 us (33%)
  starting transfers between devices  12 us (29%)
  blocking collectives  7.63 us (19%)
  other arithmetic  5.57 us (14%)
  local copies, waits for them, and re-layouts  1.57 us (4%)
    all_to_all x1, waiting for transfers between devices, body(): lax.all_to_all(masked, 'row', split_axis=1, concat_axis=0, tiled=True)  9.04 us
    all_to_all x1, starting transfers between devices, body(): lax.all_to_all(dst_local, 'row', split_axis=1, concat_axis=0, tiled=True)  8.34 us
    all_to_all x1, waiting for transfers between devices, body(): lax.all_to_all(dst_local, 'row', split_axis=1, concat_axis=0, tiled=True)  4.7 us
    all_to_all x1, blocking collectives, body(): lax.all_to_all(lax.all_to_all(masked, 'row', split_axis=1, concat_axis=0,...  3.94 us
    all_to_all x1, blocking collectives, body(): lax.all_to_all(lax.all_to_all(dst_local, 'row', split_axis=1, concat_axis...  3.69 us
    all_to_all x1, starting transfers between devices, body(): lax.all_to_all(masked, 'row', split_axis=1, concat_axis=0, tiled=True)  3.66 us
    scatter-add x1, other arithmetic, body(): jax.ops.segment_sum(received.reshape(-1, width), labels.reshape(-1), num_...  2.28 us
    mul x1, other arithmetic, body(): masked = messages * alive_mask[..., None]  1.78 us
  transfers between devices with their start and end apart: 2, of which 2 were waited for; matrix products, arithmetic and copies ran while one was open for 8% of the time, Pallas kernels for 0%

commit v1 on v0

--- a/solution.py
+++ b/solution.py
@@ -1,7 +1,40 @@
+import functools
 import jax
 import jax.numpy as jnp
 from jax import lax
 from jax.sharding import PartitionSpec as P
+
+
+def hubs_fix(field_in, axis_no, x_local):
+    h_now, low = (field_in.shape[:axis_no], field_in.shape[axis_no + 1 :])
+    mixed_arr = field_in.reshape(*h_now, x_local, -1, *low)
+    return jnp.moveaxis(mixed_arr, axis_no, 0)
+
+
+def place_halves(row_data, dim_no):
+    row_data = jnp.moveaxis(row_data, 0, dim_no)
+    y = row_data.shape
+    return row_data.reshape(*y[:dim_no], y[dim_no] * y[dim_no + 1], *y[dim_no + 2 :])
+
+
+def rails_supply_all(my_tile, which_axis, obj, block_here):
+    current_arr = lax.axis_index(which_axis)
+    arr_out = lax.axis_size(which_axis)
+    local_next, val2 = (arr_out, current_arr)
+    p_next = hubs_fix(my_tile, obj, local_next)
+    windows = [p_next[val2]]
+    j = 1
+    while j < local_next:
+        upper = p_next[val2 ^ j]
+        out_arr = lax.ppermute(upper, which_axis, [(at, at ^ j) for at in range(local_next)])
+        windows.append(out_arr)
+        j += 1
+    r_now = jnp.stack(windows, axis=0)
+    p_next = r_now[val2 ^ jnp.arange(local_next)]
+    return place_halves(p_next, block_here)
+
+
+_pass_entries = functools.partial(rails_supply_all, which_axis="row", obj=1, block_here=0)
 
 
 def body(messages, dst_local, counts, degrees):
@@ -20,13 +53,7 @@
             concat_axis=1,
             tiled=True,
         ),
-        lax.all_to_all(
-            lax.all_to_all(dst_local, "row", split_axis=1, concat_axis=0, tiled=True),
-            "col",
-            split_axis=2,
-            concat_axis=1,
-            tiled=True,
-        ),
+        lax.all_to_all(_pass_entries(dst_local), "col", split_axis=2, concat_axis=1, tiled=True),
     )
     summed = jax.ops.segment_sum(
         received.reshape(-1, width), labels.reshape(-1), num_segments=owned

time: 41 us -> 64.5 us (1.57)
  starting transfers between devices: 12 us -> 31.6 us
  waiting for transfers between devices: 13.7 us -> 16.1 us
  local copies, waits for them, and re-layouts: 1.57 us -> 3.01 us
    ppermute x0 -> x15, starting transfers between devices: none -> 27.9 us  [rails_supply_all(): lax.ppermute(upper, which_axis, [(at, at ^ j) for at in range(local_next)])]
    all_to_all x1 -> x0, starting transfers between devices: 8.34 us -> none  [body(): lax.all_to_all(dst_local, 'row', split_axis=1, concat_axis=0, tiled=True)]
    ppermute x0 -> x15, waiting for transfers between devices: none -> 7.09 us  [rails_supply_all(): lax.ppermute(upper, which_axis, [(at, at ^ j) for at in range(local_next)])]
    all_to_all x1 -> x0, waiting for transfers between devices: 4.7 us -> none  [body(): lax.all_to_all(dst_local, 'row', split_axis=1, concat_axis=0, tiled=True)]
    unnamed x6 -> x23, local copies, waits for them, and re-layouts: 0.84 us -> 1.66 us
  transfers between devices with their start and end apart: 2 -> 16, of which waited for: 2 -> 4; matrix products, arithmetic and copies ran while one was open for 8% -> 5% of each run, Pallas kernels for 0% -> 0%
where the time goes in v1:
time: 64.5 us; the launch traced here: 64 us
  starting transfers between devices  31.6 us (49%)
  waiting for transfers between devices  16.1 us (25%)
  blocking collectives  7.63 us (12%)
  other arithmetic  5.6 us (9%)
  local copies, waits for them, and re-layouts  3.01 us (5%)
    ppermute x15, starting transfers between devices, rails_supply_all(): lax.ppermute(upper, which_axis, [(at, at ^ j) for at in range(local_next)])  27.9 us
    all_to_all x1, waiting for transfers between devices, body(): lax.all_to_all(masked, 'row', split_axis=1, concat_axis=0, tiled=True)  9.04 us
    ppermute x15, waiting for transfers between devices, rails_supply_all(): lax.ppermute(upper, which_axis, [(at, at ^ j) for at in range(local_next)])  7.09 us
    all_to_all x1, blocking collectives, body(): lax.all_to_all(lax.all_to_all(masked, 'row', split_axis=1, concat_axis=0,...  3.94 us
    all_to_all x1, blocking collectives, body(): lax.all_to_all(_pass_entries(dst_local), 'col', split_axis=2, concat_axis...  3.69 us
    all_to_all x1, starting transfers between devices, body(): lax.all_to_all(masked, 'row', split_axis=1, concat_axis=0, tiled=True)  3.66 us
    scatter-add x1, other arithmetic, body(): jax.ops.segment_sum(received.reshape(-1, width), labels.reshape(-1), num_...  2.28 us
    mul x1, other arithmetic, body(): masked = messages * alive_mask[..., None]  1.79 us
  transfers between devices with their start and end apart: 16, of which 4 were waited for; matrix products, arithmetic and copies ran while one was open for 5% of the time, Pallas kernels for 0%

profile of v1, /device:TPU:0, one launch (start us, length us, event | category | flops | bytes accessed | tf_op | source)
XLA Modules:
  0.0 64.0 jit_solution(13253510728716210842)
XLA Ops:
  0.0 0.7 %copy-done = s32[1,16,2,16]{3,2,1,0:T(2,128)S(1)} copy-done((s32[1,16,2,16]{3,2,1,0:T(2,128)S(1)}, s32[1,16,2,16]{3,2,1,0:T(2,128)}, u32[]{:S(2)}) %copy-start) | copy-done | bytes 2072
  0.7 3.0 %collective-permute-start = (s32[1,1,2,16]{3,2,1,0:T(2,128)S(1)}, s32[1,1,2,16]{3,2,1,0:T(2,128)S(1)}, u32[]{:S(2)}, u32[]{:S(2)}) collective-permute-start(s32[1,1,2,16]{3,2,1,0:T(2,128)S(1)} %get-tuple-element.18), channel_id=1, source_target_pairs={{0,2},{2,0},{4,6},{6,4},{8,10},{10,8},{12,14},{14,12},{16,18},{18,... | collective-permute-start | bytes 392 | tf_op jit(solution)/shard_map/ppermute | solution.py:29
  3.8 1.5 %collective-permute-start.1 = (s32[1,1,2,16]{3,2,1,0:T(2,128)S(1)}, s32[1,1,2,16]{3,2,1,0:T(2,128)S(1)}, u32[]{:S(2)}, u32[]{:S(2)}) collective-permute-start(s32[1,1,2,16]{3,2,1,0:T(2,128)S(1)} %get-tuple-element.17), channel_id=1, source_target_pairs={{0,4},{2,6},{4,0},{6,2},{8,12},{10,14},{12,8},{14,10},{16,20},{18,... | collective-permute-start | bytes 392 | tf_op jit(solution)/shard_map/ppermute | solution.py:29
  5.3 0.0 collective-permute-start.2
  5.3 2.0 %collective-permute-start.3 = (s32[1,1,2,16]{3,2,1,0:T(2,128)S(1)}, s32[1,1,2,16]{3,2,1,0:T(2,128)S(1)}, u32[]{:S(2)}, u32[]{:S(2)}) collective-permute-start(s32[1,1,2,16]{3,2,1,0:T(2,128)S(1)} %get-tuple-element.15), channel_id=1, source_target_pairs={{0,8},{2,10},{4,12},{6,14},{8,0},{10,2},{12,4},{14,6},{16,24},{18,... | collective-permute-start | bytes 392 | tf_op jit(solution)/shard_map/ppermute | solution.py:29
  7.3 1.4 %collective-permute-start.4 = (s32[1,1,2,16]{3,2,1,0:T(2,128)S(1)}, s32[1,1,2,16]{3,2,1,0:T(2,128)S(1)}, u32[]{:S(2)}, u32[]{:S(2)}) collective-permute-start(s32[1,1,2,16]{3,2,1,0:T(2,128)S(1)} %get-tuple-element.14), channel_id=1, source_target_pairs={{0,10},{2,8},{4,14},{6,12},{8,2},{10,0},{12,6},{14,4},{16,26},{18,... | collective-permute-start | bytes 392 | tf_op jit(solution)/shard_map/ppermute | solution.py:29
  8.7 0.7 %copy-done.1 = s32[1,16,2]{1,2,0:T(2,128)S(1)} copy-done((s32[1,16,2]{1,2,0:T(2,128)S(1)}, s32[1,16,2]{1,2,0:T(2,128)}, u32[]{:S(2)}) %copy-start.1) | copy-done | bytes 152
  9.4 0.1 copy.13
  9.5 0.1 fusion.2
  9.6 1.8 %bitcast_multiply_fusion = f32[1,16,2,16,128]{4,3,2,0,1:T(8,128)} fusion(f32[1,16,2,16,128]{4,3,2,1,0:T(8,128)} %param.4, f32[16,2,16]{2,1,0:T(2,128)S(1)} %fusion.2), kind=kLoop, calls=%fused_computation.2 | loop fusion | flops 65536 | bytes 526336 | tf_op jit(solution)/shard_map/mul | solution.py:47
  11.4 0.0 collective-permute-done
  11.4 2.5 %collective-permute-start.5 = (s32[1,1,2,16]{3,2,1,0:T(2,128)S(1)}, s32[1,1,2,16]{3,2,1,0:T(2,128)S(1)}, u32[]{:S(2)}, u32[]{:S(2)}) collective-permute-start(s32[1,1,2,16]{3,2,1,0:T(2,128)S(1)} %get-tuple-element.13), channel_id=1, source_target_pairs={{0,12},{2,14},{4,8},{6,10},{8,4},{10,6},{12,0},{14,2},{16,28},{18,... | collective-permute-start | bytes 392 | tf_op jit(solution)/shard_map/ppermute | solution.py:29
  13.9 0.0 collective-permute-done.1
  13.9 0.1 collective-permute-start.6
  14.0 0.0 collective-permute-done.2
  14.0 2.9 %collective-permute-start.7 = (s32[1,1,2,16]{3,2,1,0:T(2,128)S(1)}, s32[1,1,2,16]{3,2,1,0:T(2,128)S(1)}, u32[]{:S(2)}, u32[]{:S(2)}) collective-permute-start(s32[1,1,2,16]{3,2,1,0:T(2,128)S(1)} %get-tuple-element.11), channel_id=1, source_target_pairs={{0,16},{2,18},{4,20},{6,22},{8,24},{10,26},{12,28},{14,30},{16,0},... | collective-permute-start | bytes 392 | tf_op jit(solution)/shard_map/ppermute | solution.py:29
  16.9 0.0 collective-permute-done.3
  16.9 1.3 %collective-permute-start.8 = (s32[1,1,2,16]{3,2,1,0:T(2,128)S(1)}, s32[1,1,2,16]{3,2,1,0:T(2,128)S(1)}, u32[]{:S(2)}, u32[]{:S(2)}) collective-permute-start(s32[1,1,2,16]{3,2,1,0:T(2,128)S(1)} %get-tuple-element.10), channel_id=1, source_target_pairs={{0,18},{2,16},{4,22},{6,20},{8,26},{10,24},{12,30},{14,28},{16,2},... | collective-permute-start | bytes 392 | tf_op jit(solution)/shard_map/ppermute | solution.py:29
  18.2 0.0 collective-permute-done.4
  18.2 3.5 %collective-permute-start.9 = (s32[1,1,2,16]{3,2,1,0:T(2,128)S(1)}, s32[1,1,2,16]{3,2,1,0:T(2,128)S(1)}, u32[]{:S(2)}, u32[]{:S(2)}) collective-permute-start(s32[1,1,2,16]{3,2,1,0:T(2,128)S(1)} %get-tuple-element.9), channel_id=1, source_target_pairs={{0,20},{2,22},{4,16},{6,18},{8,28},{10,30},{12,24},{14,26},{16,4},... | collective-permute-start | bytes 392 | tf_op jit(solution)/shard_map/ppermute | solution.py:29
  21.7 0.0 collective-permute-done.5
  21.7 0.1 collective-permute-start.10
  21.8 0.0 collective-permute-done.6
  21.8 3.8 %collective-permute-start.11 = (s32[1,1,2,16]{3,2,1,0:T(2,128)S(1)}, s32[1,1,2,16]{3,2,1,0:T(2,128)S(1)}, u32[]{:S(2)}, u32[]{:S(2)}) collective-permute-start(s32[1,1,2,16]{3,2,1,0:T(2,128)S(1)} %get-tuple-element.7), channel_id=1, source_target_pairs={{0,24},{2,26},{4,28},{6,30},{8,16},{10,18},{12,20},{14,22},{16,8},... | collective-permute-start | bytes 392 | tf_op jit(solution)/shard_map/ppermute | solution.py:29
  25.6 0.0 collective-permute-done.7
  25.6 1.2 %collective-permute-start.12 = (s32[1,1,2,16]{3,2,1,0:T(2,128)S(1)}, s32[1,1,2,16]{3,2,1,0:T(2,128)S(1)}, u32[]{:S(2)}, u32[]{:S(2)}) collective-permute-start(s32[1,1,2,16]{3,2,1,0:T(2,128)S(1)} %get-tuple-element.6), channel_id=1, source_target_pairs={{0,26},{2,24},{4,30},{6,28},{8,18},{10,16},{12,22},{14,20},{16,10}... | collective-permute-start | bytes 392 | tf_op jit(solution)/shard_map/ppermute | solution.py:29
  26.8 0.0 collective-permute-done.8
  26.8 4.6 %collective-permute-start.13 = (s32[1,1,2,16]{3,2,1,0:T(2,128)S(1)}, s32[1,1,2,16]{3,2,1,0:T(2,128)S(1)}, u32[]{:S(2)}, u32[]{:S(2)}) collective-permute-start(s32[1,1,2,16]{3,2,1,0:T(2,128)S(1)} %get-tuple-element.19), channel_id=1, source_target_pairs={{0,28},{2,30},{4,24},{6,26},{8,20},{10,22},{12,16},{14,18},{16,12}... | collective-permute-start | bytes 392 | tf_op jit(solution)/shard_map/ppermute | solution.py:29
  31.3 0.0 collective-permute-done.9
  31.3 0.1 collective-permute-start.14
  31.4 0.0 collective-permute-done.10
  31.4 0.0 collective-permute-done.11
  31.4 0.4 collective-permute-done.12
  31.9 1.2 %collective-permute-done.13 = s32[1,1,2,16]{3,2,1,0:T(2,128)S(1)} collective-permute-done((s32[1,1,2,16]{3,2,1,0:T(2,128)S(1)}, s32[1,1,2,16]{3,2,1,0:T(2,128)S(1)}, u32[]{:S(2)}, u32[]{:S(2)}) %collective-permute-start.13) | collective-permute-done | bytes 160 | tf_op jit(solution)/shard_map/ppermute | solution.py:29
  33.1 5.5 %collective-permute-done.14 = s32[1,1,2,16]{3,2,1,0:T(2,128)S(1)} collective-permute-done((s32[1,1,2,16]{3,2,1,0:T(2,128)S(1)}, s32[1,1,2,16]{3,2,1,0:T(2,128)S(1)}, u32[]{:S(2)}, u32[]{:S(2)}) %collective-permute-start.14) | collective-permute-done | bytes 160 | tf_op jit(solution)/shard_map/ppermute | solution.py:29
  38.5 0.6 gather_fusion
  39.1 0.1 reshape.108
  39.2 3.7 %all_to_all.30 = s32[2,1,256]{2,1,0:T(1,128)S(1)} all-to-all(s32[2,1,256]{2,1,0:T(1,128)S(1)} %reshape.108), channel_id=1, replica_groups=mesh['row'=16,'col'=2] {'col'}, dimensions={0} | all-to-all | bytes 4096 | tf_op jit(solution)/shard_map/all_to_all | solution.py:56
  42.9 3.7 %all-to-all-start.1 = ((f32[1,16,2,16,128]{4,3,2,0,1:T(8,128)}), f32[1,16,2,16,128]{4,3,2,0,1:T(8,128)S(1)}, u32[]{:S(2)}, u32[]{:S(2)}) async-start(f32[1,16,2,16,128]{4,3,2,0,1:T(8,128)} %bitcast_multiply_fusion), calls=%async_computation.1 | async-start | bytes 524288 | tf_op jit(solution)/shard_map/all_to_all | solution.py:50
  46.6 0.0 copy-done.2
  46.6 0.5 broadcast.44
  47.1 0.7 %reduce = s32[2,256]{1,0:T(2,128)S(1)} reduce(s32[2,1,256]{2,1,0:T(1,128)S(1)} %all_to_all.30, s32[]{:T(128)} %broadcast.44), dimensions={1}, to_apply=%all_to_all.8.reduce_sub_computation | reduce | bytes 4100 | tf_op jit(solution)/shard_map/all_to_all | solution.py:56
  47.8 0.1 reshape.109
  47.9 0.1 reshape.96
  47.9 9.0 %all-to-all-done.1 = f32[1,16,2,16,128]{4,3,2,0,1:T(8,128)S(1)} async-done(((f32[1,16,2,16,128]{4,3,2,0,1:T(8,128)}), f32[1,16,2,16,128]{4,3,2,0,1:T(8,128)S(1)}, u32[]{:S(2)}, u32[]{:S(2)}) %all-to-all-start.1) | async-done | bytes 262176 | tf_op jit(solution)/shard_map/all_to_all | solution.py:50
  57.0 3.9 %all_to_all.31 = f32[16,1,2,16,128]{4,3,0,1,2:T(8,128)S(1)} all-to-all(f32[16,1,2,16,128]{4,3,0,1,2:T(8,128)S(1)} %copy.15), channel_id=1, replica_groups=mesh['row'=16,'col'=2] {'col'}, dimensions={2} | all-to-all | bytes 524288 | tf_op jit(solution)/shard_map/all_to_all | solution.py:49
  61.0 2.3 %scatter_custom_fusion = f32[256,128]{1,0:T(8,128)S(1)} fusion(s32[512]{0:T(512)S(1)} %reshape.96, f32[512,128]{1,0:T(8,128)S(1)} %bitcast.50, f32[]{:T(128)} %constant.20.clone.1), kind=kCustom, calls=%fused_computation.4 | custom fusion | flops 65536 | bytes 131076 | tf_op jit(solution)/shard_map/scatter-add | solution.py:58
  63.3 0.8 %broadcast_divide_fusion = f32[256,128]{1,0:T(8,128)} fusion(f32[256,128]{1,0:T(8,128)S(1)} %scatter_custom_fusion, f32[256]{0:T(256)S(1)} %maximum_convert_fusion), kind=kLoop, calls=%fused_computation.3 | loop fusion | flops 32768 | bytes 263168 | tf_op jit(solution)/shard_map/div | solution.py:62
  (27 shorter events, 0.2 us)
Async XLA Ops:
  0.0 0.7 %copy-start = (s32[1,16,2,16]{3,2,1,0:T(2,128)S(1)}, s32[1,16,2,16]{3,2,1,0:T(2,128)}, u32[]{:S(2)}) copy-start(s32[1,16,2,16]{3,2,1,0:T(2,128)} %param.5) | copy-start | bytes 6148
  0.7 10.6 %collective-permute-start = (s32[1,1,2,16]{3,2,1,0:T(2,128)S(1)}, s32[1,1,2,16]{3,2,1,0:T(2,128)S(1)}, u32[]{:S(2)}, u32[]{:S(2)}) collective-permute-start(s32[1,1,2,16]{3,2,1,0:T(2,128)S(1)} %get-tuple-element.18), channel_id=1, source_target_pairs={{0,2},{2,0},{4,6},{6,4},{8,10},{10,8},{12,14},{14,12},{16,18},{18,... | collective-permute-start | bytes 392 | tf_op jit(solution)/shard_map/ppermute | solution.py:29
  3.8 10.2 %collective-permute-start.1 = (s32[1,1,2,16]{3,2,1,0:T(2,128)S(1)}, s32[1,1,2,16]{3,2,1,0:T(2,128)S(1)}, u32[]{:S(2)}, u32[]{:S(2)}) collective-permute-start(s32[1,1,2,16]{3,2,1,0:T(2,128)S(1)} %get-tuple-element.17), channel_id=1, source_target_pairs={{0,4},{2,6},{4,0},{6,2},{8,12},{10,14},{12,8},{14,10},{16,20},{18,... | collective-permute-start | bytes 392 | tf_op jit(solution)/shard_map/ppermute | solution.py:29
  5.3 8.7 %collective-permute-start.2 = (s32[1,1,2,16]{3,2,1,0:T(2,128)S(1)}, s32[1,1,2,16]{3,2,1,0:T(2,128)S(1)}, u32[]{:S(2)}, u32[]{:S(2)}) collective-permute-start(s32[1,1,2,16]{3,2,1,0:T(2,128)S(1)} %get-tuple-element.16), channel_id=1, source_target_pairs={{0,6},{2,4},{4,2},{6,0},{8,14},{10,12},{12,10},{14,8},{16,22},{18,... | collective-permute-start | bytes 392 | tf_op jit(solution)/shard_map/ppermute | solution.py:29
  5.3 11.6 %collective-permute-start.3 = (s32[1,1,2,16]{3,2,1,0:T(2,128)S(1)}, s32[1,1,2,16]{3,2,1,0:T(2,128)S(1)}, u32[]{:S(2)}, u32[]{:S(2)}) collective-permute-start(s32[1,1,2,16]{3,2,1,0:T(2,128)S(1)} %get-tuple-element.15), channel_id=1, source_target_pairs={{0,8},{2,10},{4,12},{6,14},{8,0},{10,2},{12,4},{14,6},{16,24},{18,... | collective-permute-start | bytes 392 | tf_op jit(solution)/shard_map/ppermute | solution.py:29
  7.3 10.8 %collective-permute-start.4 = (s32[1,1,2,16]{3,2,1,0:T(2,128)S(1)}, s32[1,1,2,16]{3,2,1,0:T(2,128)S(1)}, u32[]{:S(2)}, u32[]{:S(2)}) collective-permute-start(s32[1,1,2,16]{3,2,1,0:T(2,128)S(1)} %get-tuple-element.14), channel_id=1, source_target_pairs={{0,10},{2,8},{4,14},{6,12},{8,2},{10,0},{12,6},{14,4},{16,26},{18,... | collective-permute-start | bytes 392 | tf_op jit(solution)/shard_map/ppermute | solution.py:29
  8.7 0.7 %copy-start.1 = (s32[1,16,2]{1,2,0:T(2,128)S(1)}, s32[1,16,2]{1,2,0:T(2,128)}, u32[]{:S(2)}) copy-start(s32[1,16,2]{1,2,0:T(2,128)} %param.6) | copy-start | bytes 388
  11.4 10.4 %collective-permute-start.5 = (s32[1,1,2,16]{3,2,1,0:T(2,128)S(1)}, s32[1,1,2,16]{3,2,1,0:T(2,128)S(1)}, u32[]{:S(2)}, u32[]{:S(2)}) collective-permute-start(s32[1,1,2,16]{3,2,1,0:T(2,128)S(1)} %get-tuple-element.13), channel_id=1, source_target_pairs={{0,12},{2,14},{4,8},{6,10},{8,4},{10,6},{12,0},{14,2},{16,28},{18,... | collective-permute-start | bytes 392 | tf_op jit(solution)/shard_map/ppermute | solution.py:29
  13.9 7.9 %collective-permute-start.6 = (s32[1,1,2,16]{3,2,1,0:T(2,128)S(1)}, s32[1,1,2,16]{3,2,1,0:T(2,128)S(1)}, u32[]{:S(2)}, u32[]{:S(2)}) collective-permute-start(s32[1,1,2,16]{3,2,1,0:T(2,128)S(1)} %get-tuple-element.12), channel_id=1, source_target_pairs={{0,14},{2,12},{4,10},{6,8},{8,6},{10,4},{12,2},{14,0},{16,30},{18,... | collective-permute-start | bytes 392 | tf_op jit(solution)/shard_map/ppermute | solution.py:29
  14.0 11.6 %collective-permute-start.7 = (s32[1,1,2,16]{3,2,1,0:T(2,128)S(1)}, s32[1,1,2,16]{3,2,1,0:T(2,128)S(1)}, u32[]{:S(2)}, u32[]{:S(2)}) collective-permute-start(s32[1,1,2,16]{3,2,1,0:T(2,128)S(1)} %get-tuple-element.11), channel_id=1, source_target_pairs={{0,16},{2,18},{4,20},{6,22},{8,24},{10,26},{12,28},{14,30},{16,0},... | collective-permute-start | bytes 392 | tf_op jit(solution)/shard_map/ppermute | solution.py:29
  16.9 9.9 %collective-permute-start.8 = (s32[1,1,2,16]{3,2,1,0:T(2,128)S(1)}, s32[1,1,2,16]{3,2,1,0:T(2,128)S(1)}, u32[]{:S(2)}, u32[]{:S(2)}) collective-permute-start(s32[1,1,2,16]{3,2,1,0:T(2,128)S(1)} %get-tuple-element.10), channel_id=1, source_target_pairs={{0,18},{2,16},{4,22},{6,20},{8,26},{10,24},{12,30},{14,28},{16,2},... | collective-permute-start | bytes 392 | tf_op jit(solution)/shard_map/ppermute | solution.py:29
  18.2 13.2 %collective-permute-start.9 = (s32[1,1,2,16]{3,2,1,0:T(2,128)S(1)}, s32[1,1,2,16]{3,2,1,0:T(2,128)S(1)}, u32[]{:S(2)}, u32[]{:S(2)}) collective-permute-start(s32[1,1,2,16]{3,2,1,0:T(2,128)S(1)} %get-tuple-element.9), channel_id=1, source_target_pairs={{0,20},{2,22},{4,16},{6,18},{8,28},{10,30},{12,24},{14,26},{16,4},... | collective-permute-start | bytes 392 | tf_op jit(solution)/shard_map/ppermute | solution.py:29
  21.7 9.7 %collective-permute-start.10 = (s32[1,1,2,16]{3,2,1,0:T(2,128)S(1)}, s32[1,1,2,16]{3,2,1,0:T(2,128)S(1)}, u32[]{:S(2)}, u32[]{:S(2)}) collective-permute-start(s32[1,1,2,16]{3,2,1,0:T(2,128)S(1)} %get-tuple-element.8), channel_id=1, source_target_pairs={{0,22},{2,20},{4,18},{6,16},{8,30},{10,28},{12,26},{14,24},{16,6},... | collective-permute-start | bytes 392 | tf_op jit(solution)/shard_map/ppermute | solution.py:29
  21.8 9.6 %collective-permute-start.11 = (s32[1,1,2,16]{3,2,1,0:T(2,128)S(1)}, s32[1,1,2,16]{3,2,1,0:T(2,128)S(1)}, u32[]{:S(2)}, u32[]{:S(2)}) collective-permute-start(s32[1,1,2,16]{3,2,1,0:T(2,128)S(1)} %get-tuple-element.7), channel_id=1, source_target_pairs={{0,24},{2,26},{4,28},{6,30},{8,16},{10,18},{12,20},{14,22},{16,8},... | collective-permute-start | bytes 392 | tf_op jit(solution)/shard_map/ppermute | solution.py:29
  25.6 6.3 %collective-permute-start.12 = (s32[1,1,2,16]{3,2,1,0:T(2,128)S(1)}, s32[1,1,2,16]{3,2,1,0:T(2,128)S(1)}, u32[]{:S(2)}, u32[]{:S(2)}) collective-permute-start(s32[1,1,2,16]{3,2,1,0:T(2,128)S(1)} %get-tuple-element.6), channel_id=1, source_target_pairs={{0,26},{2,24},{4,30},{6,28},{8,18},{10,16},{12,22},{14,20},{16,10}... | collective-permute-start | bytes 392 | tf_op jit(solution)/shard_map/ppermute | solution.py:29
  26.8 6.3 %collective-permute-start.13 = (s32[1,1,2,16]{3,2,1,0:T(2,128)S(1)}, s32[1,1,2,16]{3,2,1,0:T(2,128)S(1)}, u32[]{:S(2)}, u32[]{:S(2)}) collective-permute-start(s32[1,1,2,16]{3,2,1,0:T(2,128)S(1)} %get-tuple-element.19), channel_id=1, source_target_pairs={{0,28},{2,30},{4,24},{6,26},{8,20},{10,22},{12,16},{14,18},{16,12}... | collective-permute-start | bytes 392 | tf_op jit(solution)/shard_map/ppermute | solution.py:29
  31.3 7.2 %collective-permute-start.14 = (s32[1,1,2,16]{3,2,1,0:T(2,128)S(1)}, s32[1,1,2,16]{3,2,1,0:T(2,128)S(1)}, u32[]{:S(2)}, u32[]{:S(2)}) collective-permute-start(s32[1,1,2,16]{3,2,1,0:T(2,128)S(1)} %get-tuple-element.5), channel_id=1, source_target_pairs={{0,30},{2,28},{4,26},{6,24},{8,22},{10,20},{12,18},{14,16},{16,14}... | collective-permute-start | bytes 392 | tf_op jit(solution)/shard_map/ppermute | solution.py:29
  42.9 3.7 %copy-start.2 = (s32[256]{0:T(256)S(1)}, s32[256]{0:T(256)}, u32[]{:S(2)}) copy-start(s32[256]{0:T(256)} %param.7) | copy-start | bytes 3076
  42.9 14.1 %all-to-all-start.1 = ((f32[1,16,2,16,128]{4,3,2,0,1:T(8,128)}), f32[1,16,2,16,128]{4,3,2,0,1:T(8,128)S(1)}, u32[]{:S(2)}, u32[]{:S(2)}) async-start(f32[1,16,2,16,128]{4,3,2,0,1:T(8,128)} %bitcast_multiply_fusion), calls=%async_computation.1 | async-start | bytes 524288 | tf_op jit(solution)/shard_map/all_to_all | solution.py:50
